TPU v7x, 32 devices: a whole 2x2x4 slice. The times are simulated.
32 devices in a mesh: rows: 16 (over z, y, x), cols: 2 (over core).
Axes of the slice: x: 2, y: 2, z: 4, core: 2. Of those that a mesh axis runs over, the one named last changes fastest.
Arguments:
- points: float32 [8, 4096], P(None, ('cols', 'rows')), may hold values from -6 to 6
- targets: float32 [4096], P(('cols', 'rows')), may hold values from -6 to 6
- noise: float32 [64, 4096], P(None, ('cols', 'rows')), may hold values from -6 to 6
- omega: float32 [8, 2048], P(None, 'rows'), may hold values from -12 to 12
- phase: float32 [2048], P('rows'), may hold values from -3.140625 to 3.140625
- weights: float32 [2048, 64], P('rows'), may hold values from -6 to 6
Outputs:
- posterior: float32 [64, 4096], P(None, ('cols', 'rows'))
- residual: float32 [64, 4096], P(None, ('cols', 'rows'))
All inputs are finite; a program needn't handle non-finite values.
Results may differ from a plain program's by a relative error of at most 0.02.
Values may be sent and summed in bfloat16 or wider, within the bound.
A program may use at most 64 MiB of HBM per device.

v0:
```python
import math
import jax
import jax.numpy as jnp
from jax import lax
from jax.sharding import PartitionSpec as P

ITERS = 2


def kernel_block(left, right):
    cross = lax.dot_general(
        left,
        right,
        (((0,), (0,)), ((), ())),
        precision=lax.Precision.HIGHEST,
        preferred_element_type=jnp.float32,
    )
    left_sq = jnp.sum(left * left, 0)
    right_sq = jnp.sum(right * right, 0)
    dist = left_sq[:, None] + right_sq[None, :] - 2.0 * cross
    return jnp.exp(-2.0 * dist).astype(jnp.bfloat16)


def body(points, targets, noise, omega, phase, weights):
    wide_omega, wide_phase, wide_weights = (
        lax.all_gather(omega, "rows", axis=1, tiled=True),
        lax.all_gather(phase, "rows", axis=0, tiled=True),
        lax.all_gather(weights, "rows", axis=0, tiled=True),
    )
    features = jnp.cos(
        lax.dot_general(
            wide_omega,
            points,
            (((0,), (0,)), ((), ())),
            precision=lax.Precision.HIGHEST,
            preferred_element_type=jnp.float32,
        )
        + wide_phase[:, None]
    )
    prior = math.sqrt(2.0 / wide_weights.shape[0]) * lax.dot_general(
        wide_weights,
        features,
        (((0,), (0,)), ((), ())),
        precision=lax.Precision.HIGHEST,
        preferred_element_type=jnp.float32,
    )
    rhs = targets[None, :] - prior - 0.5 * noise
    columns = lax.all_gather(points, ("rows", "cols"), axis=1, tiled=True)
    residual = rhs
    direction = rhs
    posterior = prior
    norm_now = lax.psum(jnp.sum(residual * residual, 1), ("rows", "cols"))
    for step in range(ITERS):
        low = direction.astype(jnp.bfloat16)
        kernel_part = jnp.dot(
            lax.all_gather(low, ("rows", "cols"), axis=1, tiled=True),
            kernel_block(columns, points),
            preferred_element_type=jnp.float32,
        )
        image = kernel_part + 0.25 * direction
        curve, mixed, square = lax.psum(
            (
                jnp.sum(direction * image, 1),
                jnp.sum(residual * image, 1),
                jnp.sum(image * image, 1),
            ),
            ("rows", "cols"),
        )
        alpha = norm_now / curve
        norm_next = norm_now - 2.0 * alpha * mixed + alpha * alpha * square
        posterior = posterior + alpha[:, None] * kernel_part
        residual = residual - alpha[:, None] * image
        if step + 1 < ITERS:
            direction = residual + (norm_next / norm_now)[:, None] * direction
            norm_now = norm_next
    return (posterior, residual)


def solution(mesh):
    return jax.shard_map(
        body,
        mesh=mesh,
        in_specs=(
            P(None, ("cols", "rows")),
            P(("cols", "rows")),
            P(None, ("cols", "rows")),
            P(None, "rows"),
            P("rows"),
            P("rows", None),
        ),
        out_specs=(P(None, ("cols", "rows")), P(None, ("cols", "rows"))),
        check_vma=False,
    )
```

profile of v0, /device:TPU:10, one launch (start us, length us, event | category | flops | bytes accessed | tf_op | source)
XLA Modules:
  0.0 325.9 jit_solution(18356954355384367689)
XLA Ops:
  0.6 0.0 copy-start.1
  0.6 0.0 copy-start.3
  0.7 0.0 copy-start.2
  0.7 30.7 %all_gather.18 = f32[8,2048]{1,0:T(8,128)S(1)} all-gather(f32[8,128]{1,0:T(8,128)} %param.9), channel_id=1, replica_groups=mesh['rows'=16,'cols'=2] {'rows'}, dimensions={1}, use_global_device_ids=true | all-gather | bytes 69632 | tf_op jit(solution)/shard_map/all_gather | solution.py:26
  31.3 40.7 %all-gather = f32[16,1,128]{2,1,0:T(1,128)S(1)} all-gather(f32[1,1,128]{2,1,0:T(1,128)} %bitcast.15), channel_id=1, replica_groups=mesh['rows'=16,'cols'=2] {'rows'}, dimensions={0}, use_global_device_ids=true | all-gather | bytes 8704 | tf_op jit(solution)/shard_map/all_gather | solution.py:27
  72.0 7.0 %fusion.4 = f32[2048,128]{1,0:T(8,128)S(1)} fusion(f32[8,2048]{1,0:T(8,128)S(1)} %all_gather.18, f32[8,128]{1,0:T(8,128)} %param.6, f32[2048]{0:T(1024)S(1)} %bitcast.14), kind=kOutput, calls=%fused_computation.6 | convolution fusion | flops 25427968 | bytes 1126400 | tf_op jit(solution)/shard_map/dot_general | solution.py:31
  79.1 0.0 copy-done.1
  79.1 0.0 copy-start
  79.1 38.9 %all_gather.20 = f32[2048,64]{0,1:T(8,128)S(1)} all-gather(f32[128,64]{0,1:T(8,128)S(1)} %copy-done.1), channel_id=1, replica_groups=mesh['rows'=16,'cols'=2] {'rows'}, dimensions={0}, use_global_device_ids=true | all-gather | bytes 557056 | tf_op jit(solution)/shard_map/all_gather | solution.py:28
  118.0 0.0 copy-done.3
  118.0 0.0 copy-done.2
  118.0 0.8 fusion.8
  118.8 0.0 copy-done
  118.8 38.3 %all_gather.22 = f32[8,4096]{1,0:T(8,128)S(1)} all-gather(f32[8,128]{1,0:T(8,128)S(1)} %copy-done), channel_id=1, replica_groups=mesh['rows'=16,'cols'=2] {'rows','cols'}, dimensions={1}, use_global_device_ids=true | all-gather | bytes 135168 | tf_op jit(solution)/shard_map/all_gather | solution.py:48
  157.1 3.9 %fusion.3 = bf16[4096,128]{1,0:T(8,128)(2,1)S(1)} fusion(f32[8,4096]{1,0:T(8,128)S(1)} %all_gather.22, f32[8,128]{1,0:T(8,128)S(1)} %copy-done, f32[128]{0:T(128)S(1)} %multiply_reduce_fusion.5, f32[4096]{0:T(1024)S(1)} %multiply_reduce_fusion), kind=kOutput, calls=%fused_computation.4 | convolution fusion | flops 52953088 | bytes 1200640 | tf_op jit(solution)/shard_map/dot_general | solution.py:11
  161.0 38.1 %all_gather.21 = bf16[64,4096]{1,0:T(8,128)(2,1)S(1)} all-gather(bf16[64,128]{1,0:T(8,128)(2,1)S(1)} %get-tuple-element.11), channel_id=1, replica_groups=mesh['rows'=16,'cols'=2] {'rows','cols'}, dimensions={1}, use_global_device_ids=true | all-gather | bytes 540672 | tf_op jit(solution)/shard_map/all_gather | solution.py:56
  199.1 0.4 multiply_reduce_fusion.3
  199.5 46.7 %all-reduce = (f32[64]{0:T(128)S(1)}, f32[64]{0:T(128)S(1)}, f32[64]{0:T(128)S(1)}) all-reduce(f32[64]{0:T(128)S(1)} %get-tuple-element.3, f32[64]{0:T(128)S(1)} %get-tuple-element.4, f32[64]{0:T(128)S(1)} %get-tuple-element.2), channel_id=1, replica_groups=mesh['rows'=16,'cols'=2] {'rows','cols'}, use_global_device_ids=true, to_apply=%region_7.0 | all-reduce | flops 192 | bytes 1536 | tf_op jit(solution)/shard_map/psum | solution.py:61
  246.2 0.1 fusion.6
  246.3 30.4 %all_gather.23 = bf16[64,4096]{1,0:T(8,128)(2,1)S(1)} all-gather(bf16[64,128]{1,0:T(8,128)(2,1)S(1)} %fusion.6), channel_id=1, replica_groups=mesh['rows'=16,'cols'=2] {'rows','cols'}, dimensions={1}, use_global_device_ids=true | all-gather | bytes 540672 | tf_op jit(solution)/shard_map/all_gather | solution.py:56
  276.7 0.4 multiply_reduce_fusion.1
  277.1 48.1 %psum.34 = f32[64]{0:T(128)S(1)} all-reduce(f32[64]{0:T(128)S(1)} %get-tuple-element.17), channel_id=1, replica_groups=mesh['rows'=16,'cols'=2] {'rows','cols'}, use_global_device_ids=true, to_apply=%region_9.0 | all-reduce | flops 64 | bytes 512 | tf_op jit(solution)/shard_map/psum | solution.py:61
  325.2 0.7 multiply_subtract_fusion
  (4 shorter events, 0.1 us)
Async XLA Ops:
  0.6 78.4 %copy-start.1 = (f32[128,64]{0,1:T(8,128)S(1)}, f32[128,64]{0,1:T(8,128)}, u32[]{:S(2)}) copy-start(f32[128,64]{0,1:T(8,128)} %param.11) | copy-start | bytes 98308
  0.6 117.4 %copy-start.3 = (f32[128]{0:T(128)S(1)}, f32[128]{0:T(128)}, u32[]{:S(2)}) copy-start(f32[128]{0:T(128)} %param.7) | copy-start | bytes 1540
  0.7 117.4 %copy-start.2 = (f32[64,128]{1,0:T(8,128)S(1)}, f32[64,128]{1,0:T(8,128)}, u32[]{:S(2)}) copy-start(f32[64,128]{1,0:T(8,128)} %param.8) | copy-start | bytes 98308
  79.1 39.7 %copy-start = (f32[8,128]{1,0:T(8,128)S(1)}, f32[8,128]{1,0:T(8,128)}, u32[]{:S(2)}) copy-start(f32[8,128]{1,0:T(8,128)} %param.6) | copy-start | bytes 12292
where the time goes:
time: 326 us
  blocking collectives  312 us (96%)
  matrix products  12.5 us (4%)
    psum x2, blocking collectives, body(): lax.psum((jnp.sum(direction * image, 1), jnp.sum(residual * image, 1), jn...  94.8 us
    all_gather x2, blocking collectives, body(): lax.all_gather(low, ('rows', 'cols'), axis=1, tiled=True)  68.4 us
    all_gather x1, blocking collectives, body(): lax.all_gather(phase, 'rows', axis=0, tiled=True)  40.7 us
    all_gather x1, blocking collectives, body(): lax.all_gather(weights, 'rows', axis=0, tiled=True)  38.9 us
    all_gather x1, blocking collectives, body(): columns = lax.all_gather(points, ('rows', 'cols'), axis=1, tiled=True)  38.3 us
    all_gather x1, blocking collectives, body(): lax.all_gather(omega, 'rows', axis=1, tiled=True)  30.7 us
    dot_general x1, matrix products, body(): lax.dot_general(wide_omega, points, (((0,), (0,)), ((), ())), precision=l...  7.01 us

commit v1 on v0

--- a/solution.py
+++ b/solution.py
@@ -59,12 +59,15 @@
         )
         image = kernel_part + 0.25 * direction
         curve, mixed, square = lax.psum(
-            (
-                jnp.sum(direction * image, 1),
-                jnp.sum(residual * image, 1),
-                jnp.sum(image * image, 1),
+            lax.psum(
+                (
+                    jnp.sum(direction * image, 1),
+                    jnp.sum(residual * image, 1),
+                    jnp.sum(image * image, 1),
+                ),
+                "cols",
             ),
-            ("rows", "cols"),
+            "rows",
         )
         alpha = norm_now / curve
         norm_next = norm_now - 2.0 * alpha * mixed + alpha * alpha * square

time: 326 us -> 369 us (1.13)
  the two profiles are of different devices: /device:TPU:10 before, /device:TPU:0 now
where the time goes in v1:
time: 369 us; the launch traced here: 368 us
  blocking collectives  354 us (96%)
  matrix products  12.5 us (3%)
    all_gather x2, blocking collectives, body(): lax.all_gather(low, ('rows', 'cols'), axis=1, tiled=True)  83 us
    psum x2, blocking collectives, body(): lax.psum(lax.psum((jnp.sum(direction * image, 1), jnp.sum(residual * imag...  73.1 us
    all_gather x1, blocking collectives, body(): lax.all_gather(omega, 'rows', axis=1, tiled=True)  43.1 us
    all_gather x1, blocking collectives, body(): lax.all_gather(weights, 'rows', axis=0, tiled=True)  40.4 us
    psum x1, blocking collectives, body(): norm_now = lax.psum(jnp.sum(residual * residual, 1), ('rows', 'cols'))  36.9 us
    all_gather x1, blocking collectives, body(): columns = lax.all_gather(points, ('rows', 'cols'), axis=1, tiled=True)  36.8 us
    all_gather x1, blocking collectives, body(): lax.all_gather(phase, 'rows', axis=0, tiled=True)  35.7 us

profile of v1, /device:TPU:0, one launch (start us, length us, event | category | flops | bytes accessed | tf_op | source)
XLA Modules:
  0.0 368.1 jit_solution(10869447307328696233)
XLA Ops:
  0.6 0.0 copy-start.1
  0.6 0.0 copy-start.3
  0.7 0.0 copy-start.2
  0.7 43.1 %all_gather.18 = f32[8,2048]{1,0:T(8,128)S(1)} all-gather(f32[8,128]{1,0:T(8,128)} %param.9), channel_id=1, replica_groups=mesh['rows'=16,'cols'=2] {'rows'}, dimensions={1}, use_global_device_ids=true | all-gather | bytes 69632 | tf_op jit(solution)/shard_map/all_gather | solution.py:26
  43.8 35.7 %all-gather = f32[16,1,128]{2,1,0:T(1,128)S(1)} all-gather(f32[1,1,128]{2,1,0:T(1,128)} %bitcast.15), channel_id=1, replica_groups=mesh['rows'=16,'cols'=2] {'rows'}, dimensions={0}, use_global_device_ids=true | all-gather | bytes 8704 | tf_op jit(solution)/shard_map/all_gather | solution.py:27
  79.5 7.0 %fusion.4 = f32[2048,128]{1,0:T(8,128)S(1)} fusion(f32[8,2048]{1,0:T(8,128)S(1)} %all_gather.18, f32[8,128]{1,0:T(8,128)} %param.6, f32[2048]{0:T(1024)S(1)} %bitcast.14), kind=kOutput, calls=%fused_computation.6 | convolution fusion | flops 25427968 | bytes 1126400 | tf_op jit(solution)/shard_map/dot_general | solution.py:31
  86.5 0.0 copy-done.1
  86.5 0.0 copy-start
  86.5 40.4 %all_gather.20 = f32[2048,64]{0,1:T(8,128)S(1)} all-gather(f32[128,64]{0,1:T(8,128)S(1)} %copy-done.1), channel_id=1, replica_groups=mesh['rows'=16,'cols'=2] {'rows'}, dimensions={0}, use_global_device_ids=true | all-gather | bytes 557056 | tf_op jit(solution)/shard_map/all_gather | solution.py:28
  127.0 0.0 copy-done.3
  127.0 0.8 fusion.8
  127.8 36.8 %all_gather.22 = f32[8,4096]{1,0:T(8,128)S(1)} all-gather(f32[8,128]{1,0:T(8,128)S(1)} %copy-done), channel_id=1, replica_groups=mesh['rows'=16,'cols'=2] {'rows','cols'}, dimensions={1}, use_global_device_ids=true | all-gather | bytes 135168 | tf_op jit(solution)/shard_map/all_gather | solution.py:48
  164.6 3.9 %fusion.3 = bf16[4096,128]{1,0:T(8,128)(2,1)S(1)} fusion(f32[8,4096]{1,0:T(8,128)S(1)} %all_gather.22, f32[8,128]{1,0:T(8,128)S(1)} %copy-done, f32[128]{0:T(128)S(1)} %multiply_reduce_fusion.5, f32[4096]{0:T(1024)S(1)} %multiply_reduce_fusion), kind=kOutput, calls=%fused_computation.4 | convolution fusion | flops 52953088 | bytes 1200640 | tf_op jit(solution)/shard_map/dot_general | solution.py:11
  168.5 39.8 %all_gather.21 = bf16[64,4096]{1,0:T(8,128)(2,1)S(1)} all-gather(bf16[64,128]{1,0:T(8,128)(2,1)S(1)} %get-tuple-element.12), channel_id=1, replica_groups=mesh['rows'=16,'cols'=2] {'rows','cols'}, dimensions={1}, use_global_device_ids=true | all-gather | bytes 540672 | tf_op jit(solution)/shard_map/all_gather | solution.py:56
  208.3 0.4 multiply_reduce_fusion.3
  208.8 2.5 all-reduce.1
  211.2 36.5 %all-reduce = (f32[64]{0:T(128)S(1)}, f32[64]{0:T(128)S(1)}) all-reduce(f32[64]{0:T(128)S(1)} %get-tuple-element.7, f32[64]{0:T(128)S(1)} %get-tuple-element.8), channel_id=1, replica_groups=mesh['rows'=16,'cols'=2] {'rows'}, use_global_device_ids=true, to_apply=%region_9.0 | all-reduce | flops 128 | bytes 1024 | tf_op jit(solution)/shard_map/psum | solution.py:61
  247.8 36.9 %psum.55 = f32[64]{0:T(128)S(1)} all-reduce(f32[64]{0:T(128)S(1)} %get-tuple-element.4), channel_id=1, replica_groups=mesh['rows'=16,'cols'=2] {'rows','cols'}, use_global_device_ids=true, to_apply=%region_1.0 | all-reduce | flops 64 | bytes 512 | tf_op jit(solution)/shard_map/psum | solution.py:52
  284.7 0.1 fusion.6
  284.8 43.2 %all_gather.23 = bf16[64,4096]{1,0:T(8,128)(2,1)S(1)} all-gather(bf16[64,128]{1,0:T(8,128)(2,1)S(1)} %fusion.6), channel_id=1, replica_groups=mesh['rows'=16,'cols'=2] {'rows','cols'}, dimensions={1}, use_global_device_ids=true | all-gather | bytes 540672 | tf_op jit(solution)/shard_map/all_gather | solution.py:56
  327.9 0.4 multiply_reduce_fusion.1
  328.3 2.5 psum.60
  330.8 36.5 %psum.61 = f32[64]{0:T(128)S(1)} all-reduce(f32[64]{0:T(128)S(1)} %psum.60), channel_id=1, replica_groups=mesh['rows'=16,'cols'=2] {'rows'}, use_global_device_ids=true, to_apply=%region_12.0 | all-reduce | flops 64 | bytes 512 | tf_op jit(solution)/shard_map/psum | solution.py:61
  367.4 0.7 multiply_subtract_fusion
  (6 shorter events, 0.1 us)
Async XLA Ops:
  0.6 85.9 %copy-start.1 = (f32[128,64]{0,1:T(8,128)S(1)}, f32[128,64]{0,1:T(8,128)}, u32[]{:S(2)}) copy-start(f32[128,64]{0,1:T(8,128)} %param.11) | copy-start | bytes 98308
  0.6 126.3 %copy-start.3 = (f32[128]{0:T(128)S(1)}, f32[128]{0:T(128)}, u32[]{:S(2)}) copy-start(f32[128]{0:T(128)} %param.7) | copy-start | bytes 1540
  0.7 126.3 %copy-start.2 = (f32[64,128]{1,0:T(8,128)S(1)}, f32[64,128]{1,0:T(8,128)}, u32[]{:S(2)}) copy-start(f32[64,128]{1,0:T(8,128)} %param.8) | copy-start | bytes 98308
  86.5 41.2 %copy-start = (f32[8,128]{1,0:T(8,128)S(1)}, f32[8,128]{1,0:T(8,128)}, u32[]{:S(2)}) copy-start(f32[8,128]{1,0:T(8,128)} %param.6) | copy-start | bytes 12292
